TPU v7x, 128 devices: a whole 4x4x4 slice. The times are simulated.
128 devices in a mesh: layer: 2 (over core), px: 16 (over x, z), py: 4 (over y).
Axes of the slice: x: 4, y: 4, z: 4, core: 2. Of those that a mesh axis runs over, the one named last changes fastest.
Arguments:
- right_side: float32 [8, 2048, 4096], P('layer', 'px', 'py'), may hold values from -30 to 30
- row_conduct: float32 [8, 2048, 4096], P('layer', 'px', 'py'), may hold values from 0.5 to 2
- column_conduct: float32 [8, 2048, 4096], P('layer', 'px', 'py'), may hold values from 0.5 to 2
- via_conduct: float32 [8, 2048, 4096], P('layer', 'px', 'py'), may hold values from 0.5 to 4
- via_mask: int32 [8, 2048, 4096], P('layer', 'px', 'py'), may hold values 0 or 1
- ground_conduct: float32 [8, 2048, 4096], P('layer', 'px', 'py'), may hold values from 0.01 to 0.1
Outputs:
- solution_field: float32 [8, 2048, 4096], P('layer', 'px', 'py')
- residual: float32 [8, 2048, 4096], P('layer', 'px', 'py')
All inputs are finite; a program needn't handle non-finite values. No bound on the sum of `via_mask` on one device may be relied on, other than what follows from the above.
Results may differ from a plain program's by a relative error of at most 0.0001.
Values sent between devices are 32-bit elements; how exact they have to be, the bound alone decides.
A program may use at most 128 MiB of HBM per device.

v0:
```python
import jax
import jax.numpy as jnp
from jax import lax
from jax.sharding import Mesh
from jax.sharding import PartitionSpec as P

ITERS = 2
LAYER_PX_PY = ("layer", "px_0", "px_1", "py")
PX = ("px_0", "px_1")


def extended(value, sides, width):
    edges = {}
    for axis, dim in sides:
        count, length = (lax.axis_size(axis), value.shape[dim])
        up = [(i, (i + 1) % count) for i in range(count - 1)]
        last = lax.slice_in_dim(value, length - width, length, axis=dim)
        initial = lax.slice_in_dim(value, 0, width, axis=dim)
        edges[dim] = (
            lax.ppermute(last, axis, up),
            lax.ppermute(initial, axis, [(b, a) for a, b in up]),
        )
    done = []
    for _, dim in sides:
        low, high = edges[dim]
        around = [(width, width) if d in done else (0, 0) for d in range(value.ndim)]
        value = jnp.concatenate([jnp.pad(low, around), value, jnp.pad(high, around)], axis=dim)
        done.append(dim)
    return value


def by_axis(value, axes):
    for axis in axes:
        value = lax.psum(value, axis)
    return value


def from_behind(value, axis, by):
    count = lax.axis_size(axis)
    pairs = [(i, i + by) for i in range(count) if 0 <= i + by < count]
    return lax.ppermute(value, axis, pairs)


def factor_layers(diagonal, vertical, vertical_below, carried):
    gains = []
    inverses = []
    previous = carried
    for index in range(diagonal.shape[0]):
        inverse = 1.0 / (diagonal[index] - vertical_below[index] * previous)
        previous = vertical[index] * inverse
        gains.append(previous)
        inverses.append(inverse)
    return (jnp.stack(gains), jnp.stack(inverses))


def forward_layers(residual, vertical_below, inverses, carried):
    values = []
    previous = carried
    for index in range(residual.shape[0]):
        previous = (residual[index] + vertical_below[index] * previous) * inverses[index]
        values.append(previous)
    return jnp.stack(values)


def back_layers(forward, gains, carried):
    count = forward.shape[0]
    values = [None] * count
    following = carried
    for index in range(count - 1, -1, -1):
        following = forward[index] + gains[index] * following
        values[index] = following
    return jnp.stack(values)


def operate(field, coeffs):
    diagonal, row_conduct, row_upper, column_conduct, column_left, vertical, vertical_below = coeffs
    padded = extended(field, (("layer", 0), (PX, 1), ("py", 2)), 1)
    return (
        diagonal * field
        - row_conduct * padded[1:-1, 2:, 1:-1]
        - row_upper * padded[1:-1, :-2, 1:-1]
        - column_conduct * padded[1:-1, 1:-1, 2:]
        - column_left * padded[1:-1, 1:-1, :-2]
        - vertical * padded[2:, 1:-1, 1:-1]
        - vertical_below * padded[:-2, 1:-1, 1:-1]
    )


def paired_sums(residual, precond, image):
    return (
        by_axis(jnp.sum(residual * precond), LAYER_PX_PY),
        by_axis(jnp.sum(image * precond), LAYER_PX_PY),
    )


def shards(right_side, row_conduct, column_conduct, via_conduct, via_mask, ground_conduct):
    depth = right_side.shape[0]
    members = lax.axis_size("layer")
    layers_total = depth * members
    level = lax.axis_index("layer") * depth + jnp.arange(depth, dtype=jnp.int32)
    keep = (level < layers_total - 1).astype(jnp.float32)[:, None, None]
    vertical = via_conduct * via_mask.astype(jnp.float32) * keep
    row_edge = from_behind(row_conduct[:, -1:, :], PX, 1)
    row_upper = jnp.concatenate([row_edge, row_conduct[:, :-1, :]], axis=1)
    column_edge = from_behind(column_conduct[:, :, -1:], "py", 1)
    column_left = jnp.concatenate([column_edge, column_conduct[:, :, :-1]], axis=2)
    vertical_edge = from_behind(vertical[-1:], "layer", 1)
    vertical_below = jnp.concatenate([vertical_edge, vertical[:-1]], axis=0)
    diagonal = (
        ground_conduct
        + row_conduct
        + row_upper
        + column_conduct
        + column_left
        + vertical
        + vertical_below
    )
    coeffs = (
        diagonal,
        row_conduct,
        row_upper,
        column_conduct,
        column_left,
        vertical,
        vertical_below,
    )
    plane = jnp.zeros_like(right_side[0])
    carried = plane
    gains, inverses = factor_layers(diagonal, vertical, vertical_below, carried)
    carried = from_behind(gains[-1], "layer", 1)
    gains, inverses = factor_layers(diagonal, vertical, vertical_below, carried)

    def precondition(residual):
        incoming = plane
        forward = forward_layers(residual, vertical_below, inverses, incoming)
        incoming = from_behind(forward[-1], "layer", 1)
        forward = forward_layers(residual, vertical_below, inverses, incoming)
        returning = plane
        solved = back_layers(forward, gains, returning)
        returning = from_behind(solved[0], "layer", -1)
        return back_layers(forward, gains, returning)

    solution_field = jnp.zeros_like(right_side)
    residual = right_side
    precond = precondition(residual)
    image = operate(precond, coeffs)
    rho, curvature = paired_sums(residual, precond, image)
    alpha = rho / curvature
    direction, along = (precond, image)
    for step in range(ITERS):
        solution_field = solution_field + alpha * direction
        residual = residual - alpha * along
        if step + 1 < ITERS:
            precond = precondition(residual)
            image = operate(precond, coeffs)
            rho_next, curvature = paired_sums(residual, precond, image)
            ratio = rho_next / rho
            alpha = rho_next / (curvature - ratio * rho_next / alpha)
            direction = precond + ratio * direction
            along = image + ratio * along
            rho = rho_next
    return (solution_field, residual)


def solution(mesh):
    split = Mesh(
        mesh.devices.reshape(mesh.shape["layer"], 4, 4, mesh.shape["py"]),
        ("layer", "px_0", "px_1", "py"),
    )
    return jax.shard_map(
        shards,
        mesh=split,
        in_specs=(
            P("layer", PX, "py"),
            P("layer", PX, "py"),
            P("layer", PX, "py"),
            P("layer", PX, "py"),
            P("layer", PX, "py"),
            P("layer", PX, "py"),
        ),
        out_specs=(P("layer", PX, "py"), P("layer", PX, "py")),
        check_vma=False,
    )
```

profile of v0, /device:TPU:2, one launch (start us, length us, event | category | flops | bytes accessed | tf_op | source)
XLA Modules:
  0.0 200.5 jit_solution(8595721129554607159)
XLA Ops:
  0.7 2.9 %multiply_multiply_fusion = f32[4,128,1024]{2,1,0:T(8,128)S(1)} fusion(f32[4,128,1024]{2,1,0:T(8,128)} %param.9, s32[4,128,1024]{2,1,0:T(8,128)} %param.10, f32[4]{0:T(128)S(1)} %compare_convert_fusion), kind=kLoop, calls=%fused_computation.59 | loop fusion | flops 1572864 | bytes 6291472 | tf_op jit(solution)/shard_map/mul | solution.py:102
  3.7 1.9 collective-permute-start
  5.6 3.8 %collective-permute-start.1 = (f32[4,1,1024]{2,1,0:T(1,128)S(1)}, f32[4,1,1024]{2,1,0:T(1,128)S(1)}, u32[]{:S(2)}, u32[]{:S(2)}) collective-permute-start(f32[4,1,1024]{2,1,0:T(1,128)S(1)} %slice.173), channel_id=1, source_target_pairs={{0,4},{4,8},{8,12},{12,16},{16,20},{20,24},{24,28},{28,32},{32,36}... | collective-permute-start | bytes 49160 | tf_op jit(solution)/shard_map/ppermute | solution.py:41
  9.6 3.5 %collective-permute-start.2 = (f32[4,128,1]{2,1,0:T(8,128)S(1)}, f32[4,128,1]{2,1,0:T(8,128)S(1)}, u32[]{:S(2)}, u32[]{:S(2)}) collective-permute-start(f32[4,128,1]{2,1,0:T(8,128)S(1)} %slice.175), channel_id=1, source_target_pairs={{0,1},{1,2},{2,3},{4,5},{5,6},{6,7},{8,9},{9,10},{10,11},{12,13},{... | collective-permute-start | bytes 6152 | tf_op jit(solution)/shard_map/ppermute | solution.py:41
  13.2 4.7 %collective-permute-done.2 = f32[4,128,1]{2,1,0:T(8,128)S(1)} collective-permute-done((f32[4,128,1]{2,1,0:T(8,128)S(1)}, f32[4,128,1]{2,1,0:T(8,128)S(1)}, u32[]{:S(2)}, u32[]{:S(2)}) %collective-permute-start.2) | collective-permute-done | bytes 2080 | tf_op jit(solution)/shard_map/ppermute | solution.py:41
  17.9 1.8 add_add_fusion
  24.1 2.3 %collective-permute-start.4 = (f32[128,1024]{1,0:T(8,128)S(1)}, f32[128,1024]{1,0:T(8,128)S(1)}, u32[]{:S(2)}, u32[]{:S(2)}) collective-permute-start(f32[128,1024]{1,0:T(8,128)S(1)} %get-tuple-element.40), channel_id=1, source_target_pairs={{0,64},{1,65},{2,66},{3,67},{4,68},{5,69},{6,70},{7,71},{8,72},{9,... | collective-permute-start | bytes 1572872 | tf_op jit(solution)/shard_map/ppermute | solution.py:41
  30.2 2.5 %collective-permute-done.5 = f32[128,1024]{1,0:T(8,128)S(1)} collective-permute-done((f32[128,1024]{1,0:T(8,128)S(1)}, f32[128,1024]{1,0:T(8,128)S(1)}, u32[]{:S(2)}, u32[]{:S(2)}) %collective-permute-start.5) | collective-permute-done | bytes 524320 | tf_op jit(solution)/shard_map/ppermute | solution.py:41
  33.0 2.1 %collective-permute-start.6 = (f32[1,128,1024]{2,1,0:T(8,128)S(1)}, f32[1,128,1024]{2,1,0:T(8,128)S(1)}, u32[]{:S(2)}, u32[]{:S(2)}) collective-permute-start(f32[1,128,1024]{2,1,0:T(8,128)S(1)} %bitcast.233), channel_id=1, source_target_pairs={{0,64},{1,65},{2,66},{3,67},{4,68},{5,69},{6,70},{7,71},{8,72},{9,... | collective-permute-start | bytes 1572872 | tf_op jit(solution)/shard_map/ppermute | solution.py:20
  39.1 4.0 %collective-permute-start.9 = (f32[4,1,1024]{2,1,0:T(1,128)S(1)}, f32[4,1,1024]{2,1,0:T(1,128)S(1)}, u32[]{:S(2)}, u32[]{:S(2)}) collective-permute-start(f32[4,1,1024]{2,1,0:T(1,128)S(1)} %get-tuple-element.54), channel_id=1, source_target_pairs={{0,4},{4,8},{8,12},{12,16},{16,20},{20,24},{24,28},{28,32},{32,36}... | collective-permute-start | bytes 49160 | tf_op jit(solution)/shard_map/ppermute | solution.py:20
  43.0 4.1 %collective-permute-start.8 = (f32[4,1,1024]{2,1,0:T(1,128)S(1)}, f32[4,1,1024]{2,1,0:T(1,128)S(1)}, u32[]{:S(2)}, u32[]{:S(2)}) collective-permute-start(f32[4,1,1024]{2,1,0:T(1,128)S(1)} %get-tuple-element.55), channel_id=1, source_target_pairs={{4,0},{8,4},{12,8},{16,12},{20,16},{24,20},{28,24},{32,28},{36,32}... | collective-permute-start | bytes 49160 | tf_op jit(solution)/shard_map/ppermute | solution.py:21
  48.6 5.0 %collective-permute-start.11 = (f32[4,128,1]{2,1,0:T(8,128)S(1)}, f32[4,128,1]{2,1,0:T(8,128)S(1)}, u32[]{:S(2)}, u32[]{:S(2)}) collective-permute-start(f32[4,128,1]{2,1,0:T(8,128)S(1)} %get-tuple-element.53), channel_id=1, source_target_pairs={{0,1},{1,2},{2,3},{4,5},{5,6},{6,7},{8,9},{9,10},{10,11},{12,13},{... | collective-permute-start | bytes 6152 | tf_op jit(solution)/shard_map/ppermute | solution.py:20
  54.6 4.2 %collective-permute-done.10 = f32[4,128,1]{2,1,0:T(8,128)S(1)} collective-permute-done((f32[4,128,1]{2,1,0:T(8,128)S(1)}, f32[4,128,1]{2,1,0:T(8,128)S(1)}, u32[]{:S(2)}, u32[]{:S(2)}) %collective-permute-start.10) | collective-permute-done | bytes 2080 | tf_op jit(solution)/shard_map/ppermute | solution.py:21
  60.0 9.9 %multiply_reduce_fusion.2 = (f32[]{:T(128)}, f32[]{:T(128)}, f32[4,128,1024]{2,1,0:T(8,128)}) fusion(f32[1,128,1024]{2,1,0:T(8,128)S(1)} %bitcast.235, f32[1,128,1024]{2,1,0:T(8,128)S(1)} %bitcast.245, f32[1,128,1024]{2,1,0:T(8,128)S(1)} %bitcast.242, f32[1,128,1024]{2,1,0:T(8,128)S(1)} %get-tuple-element.33, f32[4,128,1024]{2,1,0:T(8,128)S(1)} %copy-done.5, ...), kind=kLoop, calls=%fused_computation.56 | loop fusion | flops 25690112 | bytes 25219080 | tf_op jit(solution)/shard_map/reduce_sum | solution.py:92
  69.9 3.1 %all-reduce.15 = (f32[]{:T(128)}, f32[]{:T(128)}) all-reduce(f32[]{:T(128)} %get-tuple-element.5, f32[]{:T(128)} %get-tuple-element.4), channel_id=1, replica_groups=mesh['layer'=2,'px_0'=4,'px_1'=4,'py'=4] {'layer'}, use_global_device_ids=true, to_apply=%region_1.2 | all-reduce | flops 2 | bytes 16 | tf_op jit(solution)/shard_map/psum | solution.py:34
  73.0 9.3 %all-reduce.13 = (f32[]{:T(128)}, f32[]{:T(128)}) all-reduce(f32[]{:T(128)} %get-tuple-element.20, f32[]{:T(128)} %get-tuple-element.21), channel_id=1, replica_groups=mesh['layer'=2,'px_0'=4,'px_1'=4,'py'=4] {'px_0'}, use_global_device_ids=true, to_apply=%region_2.3 | all-reduce | flops 2 | bytes 16 | tf_op jit(solution)/shard_map/psum | solution.py:34
  82.3 8.7 %all-reduce.11 = (f32[]{:T(128)}, f32[]{:T(128)}) all-reduce(f32[]{:T(128)} %get-tuple-element.16, f32[]{:T(128)} %get-tuple-element.17), channel_id=1, replica_groups=mesh['layer'=2,'px_0'=4,'px_1'=4,'py'=4] {'px_1'}, use_global_device_ids=true, to_apply=%region_3.4 | all-reduce | flops 2 | bytes 16 | tf_op jit(solution)/shard_map/psum | solution.py:34
  91.0 12.8 %all-reduce.9 = (f32[]{:T(128)}, f32[]{:T(128)}) all-reduce(f32[]{:T(128)} %get-tuple-element.12, f32[]{:T(128)} %get-tuple-element.13), channel_id=1, replica_groups=mesh['layer'=2,'px_0'=4,'px_1'=4,'py'=4] {'py'}, use_global_device_ids=true, to_apply=%region_4.5 | all-reduce | flops 2 | bytes 16 | tf_op jit(solution)/shard_map/psum | solution.py:34
  105.3 2.8 %multiply_subtract_fusion.1 = f32[4,128,1024]{2,1,0:T(8,128)S(1)} fusion(f32[4,128,1024]{2,1,0:T(8,128)} %param.6, f32[4,128,1024]{2,1,0:T(8,128)} %get-tuple-element.31, f32[]{:T(128)S(6)} %div.44), kind=kLoop, calls=%fused_computation.55 | loop fusion | flops 1048576 | bytes 6291460 | tf_op jit(solution)/shard_map/sub | solution.py:152
  108.8 1.6 collective-permute-start.12
  114.1 2.5 %collective-permute-done.13 = f32[128,1024]{1,0:T(8,128)S(1)} collective-permute-done((f32[128,1024]{1,0:T(8,128)S(1)}, f32[128,1024]{1,0:T(8,128)S(1)}, u32[]{:S(2)}, u32[]{:S(2)}) %collective-permute-start.13) | collective-permute-done | bytes 524320 | tf_op jit(solution)/shard_map/ppermute | solution.py:41
  116.9 2.1 %collective-permute-start.14 = (f32[1,128,1024]{2,1,0:T(8,128)S(1)}, f32[1,128,1024]{2,1,0:T(8,128)S(1)}, u32[]{:S(2)}, u32[]{:S(2)}) collective-permute-start(f32[1,128,1024]{2,1,0:T(8,128)S(1)} %bitcast.237), channel_id=1, source_target_pairs={{0,64},{1,65},{2,66},{3,67},{4,68},{5,69},{6,70},{7,71},{8,72},{9,... | collective-permute-start | bytes 1572872 | tf_op jit(solution)/shard_map/ppermute | solution.py:20
  125.8 3.9 %collective-permute-start.17 = (f32[4,1,1024]{2,1,0:T(1,128)S(1)}, f32[4,1,1024]{2,1,0:T(1,128)S(1)}, u32[]{:S(2)}, u32[]{:S(2)}) collective-permute-start(f32[4,1,1024]{2,1,0:T(1,128)S(1)} %get-tuple-element.50), channel_id=1, source_target_pairs={{0,4},{4,8},{8,12},{12,16},{16,20},{20,24},{24,28},{28,32},{32,36}... | collective-permute-start | bytes 49160 | tf_op jit(solution)/shard_map/ppermute | solution.py:20
  129.7 4.3 %collective-permute-start.16 = (f32[4,1,1024]{2,1,0:T(1,128)S(1)}, f32[4,1,1024]{2,1,0:T(1,128)S(1)}, u32[]{:S(2)}, u32[]{:S(2)}) collective-permute-start(f32[4,1,1024]{2,1,0:T(1,128)S(1)} %get-tuple-element.51), channel_id=1, source_target_pairs={{4,0},{8,4},{12,8},{16,12},{20,16},{24,20},{28,24},{32,28},{36,32}... | collective-permute-start | bytes 49160 | tf_op jit(solution)/shard_map/ppermute | solution.py:21
  136.4 4.6 %collective-permute-start.19 = (f32[4,128,1]{2,1,0:T(8,128)S(1)}, f32[4,128,1]{2,1,0:T(8,128)S(1)}, u32[]{:S(2)}, u32[]{:S(2)}) collective-permute-start(f32[4,128,1]{2,1,0:T(8,128)S(1)} %get-tuple-element.49), channel_id=1, source_target_pairs={{0,1},{1,2},{2,3},{4,5},{5,6},{6,7},{8,9},{9,10},{10,11},{12,13},{... | collective-permute-start | bytes 6152 | tf_op jit(solution)/shard_map/ppermute | solution.py:20
  141.8 3.9 %collective-permute-done.18 = f32[4,128,1]{2,1,0:T(8,128)S(1)} collective-permute-done((f32[4,128,1]{2,1,0:T(8,128)S(1)}, f32[4,128,1]{2,1,0:T(8,128)S(1)}, u32[]{:S(2)}, u32[]{:S(2)}) %collective-permute-start.18) | collective-permute-done | bytes 2080 | tf_op jit(solution)/shard_map/ppermute | solution.py:21
  147.0 10.1 %multiply_reduce_fusion = (f32[]{:T(128)}, f32[]{:T(128)}, f32[4,128,1024]{2,1,0:T(8,128)}) fusion(f32[1,128,1024]{2,1,0:T(8,128)S(1)} %bitcast.239, f32[1,128,1024]{2,1,0:T(8,128)S(1)} %bitcast.251, f32[1,128,1024]{2,1,0:T(8,128)S(1)} %bitcast.248, f32[1,128,1024]{2,1,0:T(8,128)S(1)} %get-tuple-element.24, f32[4,128,1024]{2,1,0:T(8,128)S(1)} %multiply_subtract_fusion.1, ...), kind=kLoop, calls=%fused_computation.53 | loop fusion | flops 25690112 | bytes 25219080 | tf_op jit(solution)/shard_map/reduce_sum | solution.py:92
  157.1 3.1 %all-reduce.14 = (f32[]{:T(128)}, f32[]{:T(128)}) all-reduce(f32[]{:T(128)} %get-tuple-element.3, f32[]{:T(128)} %get-tuple-element.2), channel_id=1, replica_groups=mesh['layer'=2,'px_0'=4,'px_1'=4,'py'=4] {'layer'}, use_global_device_ids=true, to_apply=%region_11.12 | all-reduce | flops 2 | bytes 16 | tf_op jit(solution)/shard_map/psum | solution.py:34
  160.2 9.0 %all-reduce.12 = (f32[]{:T(128)}, f32[]{:T(128)}) all-reduce(f32[]{:T(128)} %get-tuple-element.18, f32[]{:T(128)} %get-tuple-element.19), channel_id=1, replica_groups=mesh['layer'=2,'px_0'=4,'px_1'=4,'py'=4] {'px_0'}, use_global_device_ids=true, to_apply=%region_12.13 | all-reduce | flops 2 | bytes 16 | tf_op jit(solution)/shard_map/psum | solution.py:34
  169.1 9.8 %all-reduce.10 = (f32[]{:T(128)}, f32[]{:T(128)}) all-reduce(f32[]{:T(128)} %get-tuple-element.14, f32[]{:T(128)} %get-tuple-element.15), channel_id=1, replica_groups=mesh['layer'=2,'px_0'=4,'px_1'=4,'py'=4] {'px_1'}, use_global_device_ids=true, to_apply=%region_13.14 | all-reduce | flops 2 | bytes 16 | tf_op jit(solution)/shard_map/psum | solution.py:34
  178.9 10.9 %all-reduce.8 = (f32[]{:T(128)}, f32[]{:T(128)}) all-reduce(f32[]{:T(128)} %get-tuple-element.10, f32[]{:T(128)} %get-tuple-element.11), channel_id=1, replica_groups=mesh['layer'=2,'px_0'=4,'px_1'=4,'py'=4] {'py'}, use_global_device_ids=true, to_apply=%region_14.15 | all-reduce | flops 2 | bytes 16 | tf_op jit(solution)/shard_map/psum | solution.py:34
  194.4 6.0 %multiply_subtract_fusion = (f32[4,128,1024]{2,1,0:T(8,128)}, f32[4,128,1024]{2,1,0:T(8,128)}) fusion(f32[4,128,1024]{2,1,0:T(8,128)} %copy-done.4, f32[4,128,1024]{2,1,0:T(8,128)} %get-tuple-element.22, f32[4,128,1024]{2,1,0:T(8,128)} %get-tuple-element.31, f32[]{:T(128)S(6)} %div.45, f32[]{:T(128)S(6)} %div.47, f32[1,128,1024]{2,1,0:T(8,128)} %bitcast.240, ...), kind=kLoop, calls=%fused_computation.51 | loop fusion | flops 7864320 | bytes 14680076 | tf_op jit(solution)/shard_map/sub | solution.py:152
  (124 shorter events, 31.8 us)
Async XLA Ops:
  3.7 14.2 %collective-permute-start = (f32[1,128,1024]{2,1,0:T(8,128)S(1)}, f32[1,128,1024]{2,1,0:T(8,128)S(1)}, u32[]{:S(2)}, u32[]{:S(2)}) collective-permute-start(f32[1,128,1024]{2,1,0:T(8,128)S(1)} %slice.202), channel_id=1, source_target_pairs={{0,64},{1,65},{2,66},{3,67},{4,68},{5,69},{6,70},{7,71},{8,72},{9,... | collective-permute-start | bytes 1572872 | tf_op jit(solution)/shard_map/ppermute | solution.py:41
  5.6 12.3 %collective-permute-start.1 = (f32[4,1,1024]{2,1,0:T(1,128)S(1)}, f32[4,1,1024]{2,1,0:T(1,128)S(1)}, u32[]{:S(2)}, u32[]{:S(2)}) collective-permute-start(f32[4,1,1024]{2,1,0:T(1,128)S(1)} %slice.173), channel_id=1, source_target_pairs={{0,4},{4,8},{8,12},{12,16},{16,20},{20,24},{24,28},{28,32},{32,36}... | collective-permute-start | bytes 49160 | tf_op jit(solution)/shard_map/ppermute | solution.py:41
  9.6 8.3 %collective-permute-start.2 = (f32[4,128,1]{2,1,0:T(8,128)S(1)}, f32[4,128,1]{2,1,0:T(8,128)S(1)}, u32[]{:S(2)}, u32[]{:S(2)}) collective-permute-start(f32[4,128,1]{2,1,0:T(8,128)S(1)} %slice.175), channel_id=1, source_target_pairs={{0,1},{1,2},{2,3},{4,5},{5,6},{6,7},{8,9},{9,10},{10,11},{12,13},{... | collective-permute-start | bytes 6152 | tf_op jit(solution)/shard_map/ppermute | solution.py:41
  13.2 46.7 %copy-start.6 = (f32[3,128,1024]{2,1,0:T(8,128)}, f32[3,128,1024]{2,1,0:T(8,128)S(1)}, u32[]{:S(2)}) copy-start(f32[3,128,1024]{2,1,0:T(8,128)S(1)} %slice.206) | copy-start | bytes 4718596
  20.2 2.9 %collective-permute-start.3 = (f32[128,1024]{1,0:T(8,128)S(1)}, f32[128,1024]{1,0:T(8,128)S(1)}, u32[]{:S(2)}, u32[]{:S(2)}) collective-permute-start(f32[128,1024]{1,0:T(8,128)S(1)} %fusion.30), channel_id=1, source_target_pairs={{0,64},{1,65},{2,66},{3,67},{4,68},{5,69},{6,70},{7,71},{8,72},{9,... | collective-permute-start | bytes 1572872 | tf_op jit(solution)/shard_map/ppermute | solution.py:41
  24.1 3.8 %collective-permute-start.4 = (f32[128,1024]{1,0:T(8,128)S(1)}, f32[128,1024]{1,0:T(8,128)S(1)}, u32[]{:S(2)}, u32[]{:S(2)}) collective-permute-start(f32[128,1024]{1,0:T(8,128)S(1)} %get-tuple-element.40), channel_id=1, source_target_pairs={{0,64},{1,65},{2,66},{3,67},{4,68},{5,69},{6,70},{7,71},{8,72},{9,... | collective-permute-start | bytes 1572872 | tf_op jit(solution)/shard_map/ppermute | solution.py:41
  28.9 3.8 %collective-permute-start.5 = (f32[128,1024]{1,0:T(8,128)S(1)}, f32[128,1024]{1,0:T(8,128)S(1)}, u32[]{:S(2)}, u32[]{:S(2)}) collective-permute-start(f32[128,1024]{1,0:T(8,128)S(1)} %get-tuple-element.36), channel_id=1, source_target_pairs={{64,0},{65,1},{66,2},{67,3},{68,4},{69,5},{70,6},{71,7},{72,8},{73... | collective-permute-start | bytes 1572872 | tf_op jit(solution)/shard_map/ppermute | solution.py:41
  33.0 3.6 %collective-permute-start.6 = (f32[1,128,1024]{2,1,0:T(8,128)S(1)}, f32[1,128,1024]{2,1,0:T(8,128)S(1)}, u32[]{:S(2)}, u32[]{:S(2)}) collective-permute-start(f32[1,128,1024]{2,1,0:T(8,128)S(1)} %bitcast.233), channel_id=1, source_target_pairs={{0,64},{1,65},{2,66},{3,67},{4,68},{5,69},{6,70},{7,71},{8,72},{9,... | collective-permute-start | bytes 1572872 | tf_op jit(solution)/shard_map/ppermute | solution.py:20
  37.4 22.6 %copy-start.13 = (f32[128,1024]{1,0:T(8,128)}, f32[128,1024]{1,0:T(8,128)S(1)}, u32[]{:S(2)}) copy-start(f32[128,1024]{1,0:T(8,128)S(1)} %get-tuple-element.34) | copy-start | bytes 1572868
  37.4 22.6 %copy-start.14 = (f32[128,1024]{1,0:T(8,128)}, f32[128,1024]{1,0:T(8,128)S(1)}, u32[]{:S(2)}) copy-start(f32[128,1024]{1,0:T(8,128)S(1)} %get-tuple-element.35) | copy-start | bytes 1572868
  37.4 22.6 %copy-start.23 = (f32[1,128,1024]{2,1,0:T(8,128)}, f32[1,128,1024]{2,1,0:T(8,128)S(1)}, u32[]{:S(2)}) copy-start(f32[1,128,1024]{2,1,0:T(8,128)S(1)} %get-tuple-element.33) | copy-start | bytes 1572868
  37.4 16.4 %collective-permute-start.7 = (f32[1,128,1024]{2,1,0:T(8,128)S(1)}, f32[1,128,1024]{2,1,0:T(8,128)S(1)}, u32[]{:S(2)}, u32[]{:S(2)}) collective-permute-start(f32[1,128,1024]{2,1,0:T(8,128)S(1)} %get-tuple-element.33), channel_id=1, source_target_pairs={{64,0},{65,1},{66,2},{67,3},{68,4},{69,5},{70,6},{71,7},{72,8},{73... | collective-permute-start | bytes 1572872 | tf_op jit(solution)/shard_map/ppermute | solution.py:21
  39.1 14.6 %collective-permute-start.9 = (f32[4,1,1024]{2,1,0:T(1,128)S(1)}, f32[4,1,1024]{2,1,0:T(1,128)S(1)}, u32[]{:S(2)}, u32[]{:S(2)}) collective-permute-start(f32[4,1,1024]{2,1,0:T(1,128)S(1)} %get-tuple-element.54), channel_id=1, source_target_pairs={{0,4},{4,8},{8,12},{12,16},{16,20},{20,24},{24,28},{28,32},{32,36}... | collective-permute-start | bytes 49160 | tf_op jit(solution)/shard_map/ppermute | solution.py:20
  43.0 10.7 %collective-permute-start.8 = (f32[4,1,1024]{2,1,0:T(1,128)S(1)}, f32[4,1,1024]{2,1,0:T(1,128)S(1)}, u32[]{:S(2)}, u32[]{:S(2)}) collective-permute-start(f32[4,1,1024]{2,1,0:T(1,128)S(1)} %get-tuple-element.55), channel_id=1, source_target_pairs={{4,0},{8,4},{12,8},{16,12},{20,16},{24,20},{28,24},{32,28},{36,32}... | collective-permute-start | bytes 49160 | tf_op jit(solution)/shard_map/ppermute | solution.py:21
  47.3 11.4 %collective-permute-start.10 = (f32[4,128,1]{2,1,0:T(8,128)S(1)}, f32[4,128,1]{2,1,0:T(8,128)S(1)}, u32[]{:S(2)}, u32[]{:S(2)}) collective-permute-start(f32[4,128,1]{2,1,0:T(8,128)S(1)} %get-tuple-element.52), channel_id=1, source_target_pairs={{1,0},{2,1},{3,2},{5,4},{6,5},{7,6},{9,8},{10,9},{11,10},{13,12},{... | collective-permute-start | bytes 6152 | tf_op jit(solution)/shard_map/ppermute | solution.py:21
  48.6 11.3 %collective-permute-start.11 = (f32[4,128,1]{2,1,0:T(8,128)S(1)}, f32[4,128,1]{2,1,0:T(8,128)S(1)}, u32[]{:S(2)}, u32[]{:S(2)}) collective-permute-start(f32[4,128,1]{2,1,0:T(8,128)S(1)} %get-tuple-element.53), channel_id=1, source_target_pairs={{0,1},{1,2},{2,3},{4,5},{5,6},{6,7},{8,9},{9,10},{10,11},{12,13},{... | collective-permute-start | bytes 6152 | tf_op jit(solution)/shard_map/ppermute | solution.py:20
  108.1 38.8 %copy-start.4 = (f32[4,128,1024]{2,1,0:T(8,128)}, f32[4,128,1024]{2,1,0:T(8,128)S(1)}, u32[]{:S(2)}) copy-start(f32[4,128,1024]{2,1,0:T(8,128)S(1)} %multiply_subtract_fusion.1) | copy-start | bytes 6291460
  108.8 2.9 %collective-permute-start.12 = (f32[128,1024]{1,0:T(8,128)S(1)}, f32[128,1024]{1,0:T(8,128)S(1)}, u32[]{:S(2)}, u32[]{:S(2)}) collective-permute-start(f32[128,1024]{1,0:T(8,128)S(1)} %add_multiply_fusion.3), channel_id=1, source_target_pairs={{0,64},{1,65},{2,66},{3,67},{4,68},{5,69},{6,70},{7,71},{8,72},{9,... | collective-permute-start | bytes 1572872 | tf_op jit(solution)/shard_map/ppermute | solution.py:41
  112.8 3.8 %collective-permute-start.13 = (f32[128,1024]{1,0:T(8,128)S(1)}, f32[128,1024]{1,0:T(8,128)S(1)}, u32[]{:S(2)}, u32[]{:S(2)}) collective-permute-start(f32[128,1024]{1,0:T(8,128)S(1)} %get-tuple-element.27), channel_id=1, source_target_pairs={{64,0},{65,1},{66,2},{67,3},{68,4},{69,5},{70,6},{71,7},{72,8},{73... | collective-permute-start | bytes 1572872 | tf_op jit(solution)/shard_map/ppermute | solution.py:41
  116.9 30.1 %copy-start.10 = (f32[128,1024]{1,0:T(8,128)}, f32[128,1024]{1,0:T(8,128)S(1)}, u32[]{:S(2)}) copy-start(f32[128,1024]{1,0:T(8,128)S(1)} %multiply_add_fusion.3) | copy-start | bytes 1572868
  116.9 3.6 %collective-permute-start.14 = (f32[1,128,1024]{2,1,0:T(8,128)S(1)}, f32[1,128,1024]{2,1,0:T(8,128)S(1)}, u32[]{:S(2)}, u32[]{:S(2)}) collective-permute-start(f32[1,128,1024]{2,1,0:T(8,128)S(1)} %bitcast.237), channel_id=1, source_target_pairs={{0,64},{1,65},{2,66},{3,67},{4,68},{5,69},{6,70},{7,71},{8,72},{9,... | collective-permute-start | bytes 1572872 | tf_op jit(solution)/shard_map/ppermute | solution.py:20
  122.6 24.4 %copy-start.15 = (f32[128,1024]{1,0:T(8,128)}, f32[128,1024]{1,0:T(8,128)S(1)}, u32[]{:S(2)}) copy-start(f32[128,1024]{1,0:T(8,128)S(1)} %get-tuple-element.25) | copy-start | bytes 1572868
  122.6 24.4 %copy-start.16 = (f32[128,1024]{1,0:T(8,128)}, f32[128,1024]{1,0:T(8,128)S(1)}, u32[]{:S(2)}) copy-start(f32[128,1024]{1,0:T(8,128)S(1)} %get-tuple-element.26) | copy-start | bytes 1572868
  122.6 24.4 %copy-start.24 = (f32[1,128,1024]{2,1,0:T(8,128)}, f32[1,128,1024]{2,1,0:T(8,128)S(1)}, u32[]{:S(2)}) copy-start(f32[1,128,1024]{2,1,0:T(8,128)S(1)} %get-tuple-element.24) | copy-start | bytes 1572868
  122.6 18.4 %collective-permute-start.15 = (f32[1,128,1024]{2,1,0:T(8,128)S(1)}, f32[1,128,1024]{2,1,0:T(8,128)S(1)}, u32[]{:S(2)}, u32[]{:S(2)}) collective-permute-start(f32[1,128,1024]{2,1,0:T(8,128)S(1)} %get-tuple-element.24), channel_id=1, source_target_pairs={{64,0},{65,1},{66,2},{67,3},{68,4},{69,5},{70,6},{71,7},{72,8},{73... | collective-permute-start | bytes 1572872 | tf_op jit(solution)/shard_map/ppermute | solution.py:21
  124.7 22.3 %copy-start.9 = (f32[4,128,1024]{2,1,0:T(8,128)S(1)}, f32[4,128,1024]{2,1,0:T(8,128)}, u32[]{:S(2)}) copy-start(f32[4,128,1024]{2,1,0:T(8,128)} %param.11) | copy-start | bytes 6291460
  125.5 21.4 %copy-start.3 = (f32[4,128,1024]{2,1,0:T(8,128)S(1)}, f32[4,128,1024]{2,1,0:T(8,128)}, u32[]{:S(2)}) copy-start(f32[4,128,1024]{2,1,0:T(8,128)} %param.7) | copy-start | bytes 6291460
  125.5 21.4 %copy-start.7 = (f32[3,128,1024]{2,1,0:T(8,128)S(1)}, f32[3,128,1024]{2,1,0:T(8,128)}, u32[]{:S(2)}) copy-start(f32[3,128,1024]{2,1,0:T(8,128)} %copy-done.6) | copy-start | bytes 4718596
  125.8 15.1 %collective-permute-start.17 = (f32[4,1,1024]{2,1,0:T(1,128)S(1)}, f32[4,1,1024]{2,1,0:T(1,128)S(1)}, u32[]{:S(2)}, u32[]{:S(2)}) collective-permute-start(f32[4,1,1024]{2,1,0:T(1,128)S(1)} %get-tuple-element.50), channel_id=1, source_target_pairs={{0,4},{4,8},{8,12},{12,16},{16,20},{20,24},{24,28},{28,32},{32,36}... | collective-permute-start | bytes 49160 | tf_op jit(solution)/shard_map/ppermute | solution.py:20
  129.7 11.2 %collective-permute-start.16 = (f32[4,1,1024]{2,1,0:T(1,128)S(1)}, f32[4,1,1024]{2,1,0:T(1,128)S(1)}, u32[]{:S(2)}, u32[]{:S(2)}) collective-permute-start(f32[4,1,1024]{2,1,0:T(1,128)S(1)} %get-tuple-element.51), channel_id=1, source_target_pairs={{4,0},{8,4},{12,8},{16,12},{20,16},{24,20},{28,24},{32,28},{36,32}... | collective-permute-start | bytes 49160 | tf_op jit(solution)/shard_map/ppermute | solution.py:21
  135.1 10.7 %collective-permute-start.18 = (f32[4,128,1]{2,1,0:T(8,128)S(1)}, f32[4,128,1]{2,1,0:T(8,128)S(1)}, u32[]{:S(2)}, u32[]{:S(2)}) collective-permute-start(f32[4,128,1]{2,1,0:T(8,128)S(1)} %get-tuple-element.48), channel_id=1, source_target_pairs={{1,0},{2,1},{3,2},{5,4},{6,5},{7,6},{9,8},{10,9},{11,10},{13,12},{... | collective-permute-start | bytes 6152 | tf_op jit(solution)/shard_map/ppermute | solution.py:21
  136.4 10.6 %collective-permute-start.19 = (f32[4,128,1]{2,1,0:T(8,128)S(1)}, f32[4,128,1]{2,1,0:T(8,128)S(1)}, u32[]{:S(2)}, u32[]{:S(2)}) collective-permute-start(f32[4,128,1]{2,1,0:T(8,128)S(1)} %get-tuple-element.49), channel_id=1, source_target_pairs={{0,1},{1,2},{2,3},{4,5},{5,6},{6,7},{8,9},{9,10},{10,11},{12,13},{... | collective-permute-start | bytes 6152 | tf_op jit(solution)/shard_map/ppermute | solution.py:20
  (22 other events, 158.5 us)
where the time goes:
time: 201 us
  blocking collectives  66.7 us (33%)
  starting transfers between devices  52.4 us (26%)
  other arithmetic  40.2 us (20%)
  waiting for transfers between devices  27.4 us (14%)
  between operations  7.53 us (4%)
  local copies, waits for them, and re-layouts  6.31 us (3%)
    psum x8, blocking collectives, by_axis(): value = lax.psum(value, axis)  66.7 us
    ppermute x6, starting transfers between devices, extended(): lax.ppermute(last, axis, up)  21.6 us
    reduce_sum x2, other arithmetic, paired_sums(): jnp.sum(image * precond)  20 us
    ppermute x8, starting transfers between devices, from_behind(): return lax.ppermute(value, axis, pairs)  17.2 us
    ppermute x8, waiting for transfers between devices, from_behind(): return lax.ppermute(value, axis, pairs)  13.9 us
    ppermute x6, starting transfers between devices, extended(): lax.ppermute(initial, axis, [(b, a) for a, b in up])  13.6 us
    sub x2, other arithmetic, shards(): residual = residual - alpha * along  8.84 us
    ppermute x6, waiting for transfers between devices, extended(): lax.ppermute(initial, axis, [(b, a) for a, b in up])  8.16 us
  transfers between devices with their start and end apart: 20, of which 12 were waited for; matrix products, arithmetic and copies ran while one was open for 2% of the time, Pallas kernels for 0%

commit v1 on v0

--- a/solution.py
+++ b/solution.py
@@ -31,7 +31,8 @@
 
 def by_axis(value, axes):
     for axis in axes:
-        value = lax.psum(value, axis)
+        shards_2 = lax.all_gather(value, axis, axis=0, tiled=False)
+        value = shards_2.sum(axis=0)
     return value
 
 

time: 201 us -> 231 us (1.15)
  local copies, waits for them, and re-layouts: 6.31 us -> 26.9 us
  other arithmetic: 40.2 us -> 51.1 us
  starting transfers between devices: 52.4 us -> 49.4 us
    psum x8 -> x0, blocking collectives: 66.7 us -> none  [by_axis(): value = lax.psum(value, axis)]
    unnamed x0 -> x8, blocking collectives: none -> 66 us
    unnamed x76 -> x126, local copies, waits for them, and re-layouts: 4.74 us -> 26.1 us
    reduce_sum x0 -> x16, other arithmetic: none -> 10.6 us  [by_axis(): value = shards_2.sum(axis=0)]
  transfers between devices with their start and end apart: 20 -> 20, of which waited for: 12 -> 12; matrix products, arithmetic and copies ran while one was open for 2% -> 1% of each run, Pallas kernels for 0% -> 0%
where the time goes in v1:
time: 231 us; the launch traced here: 229 us
  blocking collectives  66 us (29%)
  other arithmetic  51.1 us (22%)
  starting transfers between devices  49.4 us (21%)
  waiting for transfers between devices  28.1 us (12%)
  local copies, waits for them, and re-layouts  26.9 us (12%)
  between operations  7.49 us (3%)
    unnamed x8, blocking collectives  66 us
    unnamed x126, local copies, waits for them, and re-layouts  26.1 us
    ppermute x6, starting transfers between devices, extended(): lax.ppermute(last, axis, up)  19.9 us
    reduce_sum x2, other arithmetic, paired_sums(): jnp.sum(image * precond)  18.3 us
    ppermute x8, starting transfers between devices, from_behind(): return lax.ppermute(value, axis, pairs)  17.2 us
    ppermute x8, waiting for transfers between devices, from_behind(): return lax.ppermute(value, axis, pairs)  14.1 us
    ppermute x6, starting transfers between devices, extended(): lax.ppermute(initial, axis, [(b, a) for a, b in up])  12.4 us
    reduce_sum x16, other arithmetic, by_axis(): value = shards_2.sum(axis=0)  10.6 us
  transfers between devices with their start and end apart: 20, of which 12 were waited for; matrix products, arithmetic and copies ran while one was open for 1% of the time, Pallas kernels for 0%

profile of v1, /device:TPU:2, one launch (start us, length us, event | category | flops | bytes accessed | tf_op | source)
XLA Modules:
  0.0 229.0 jit_solution(15398812846438519659)
XLA Ops:
  0.7 3.1 %multiply_multiply_fusion = f32[4,128,1024]{2,1,0:T(8,128)S(1)} fusion(f32[4,128,1024]{2,1,0:T(8,128)} %param.9, s32[4,128,1024]{2,1,0:T(8,128)} %param.10, f32[4]{0:T(128)S(1)} %compare_convert_fusion), kind=kLoop, calls=%fused_computation.59 | loop fusion | flops 1572864 | bytes 6291472 | tf_op jit(solution)/shard_map/mul | solution.py:103
  3.8 1.9 collective-permute-start
  5.8 3.8 %collective-permute-start.1 = (f32[4,1,1024]{2,1,0:T(1,128)S(1)}, f32[4,1,1024]{2,1,0:T(1,128)S(1)}, u32[]{:S(2)}, u32[]{:S(2)}) collective-permute-start(f32[4,1,1024]{2,1,0:T(1,128)S(1)} %slice.173), channel_id=1, source_target_pairs={{0,4},{4,8},{8,12},{12,16},{16,20},{20,24},{24,28},{28,32},{32,36}... | collective-permute-start | bytes 49160 | tf_op jit(solution)/shard_map/ppermute | solution.py:42
  9.7 3.5 %collective-permute-start.2 = (f32[4,128,1]{2,1,0:T(8,128)S(1)}, f32[4,128,1]{2,1,0:T(8,128)S(1)}, u32[]{:S(2)}, u32[]{:S(2)}) collective-permute-start(f32[4,128,1]{2,1,0:T(8,128)S(1)} %slice.175), channel_id=1, source_target_pairs={{0,1},{1,2},{2,3},{4,5},{5,6},{6,7},{8,9},{9,10},{10,11},{12,13},{... | collective-permute-start | bytes 6152 | tf_op jit(solution)/shard_map/ppermute | solution.py:42
  13.4 4.7 %collective-permute-done.2 = f32[4,128,1]{2,1,0:T(8,128)S(1)} collective-permute-done((f32[4,128,1]{2,1,0:T(8,128)S(1)}, f32[4,128,1]{2,1,0:T(8,128)S(1)}, u32[]{:S(2)}, u32[]{:S(2)}) %collective-permute-start.2) | collective-permute-done | bytes 2080 | tf_op jit(solution)/shard_map/ppermute | solution.py:42
  24.1 2.3 %collective-permute-start.4 = (f32[128,1024]{1,0:T(8,128)S(1)}, f32[128,1024]{1,0:T(8,128)S(1)}, u32[]{:S(2)}, u32[]{:S(2)}) collective-permute-start(f32[128,1024]{1,0:T(8,128)S(1)} %get-tuple-element.40), channel_id=1, source_target_pairs={{0,64},{1,65},{2,66},{3,67},{4,68},{5,69},{6,70},{7,71},{8,72},{9,... | collective-permute-start | bytes 1572872 | tf_op jit(solution)/shard_map/ppermute | solution.py:42
  27.9 2.0 multiply_add_fusion.8
  31.4 2.5 %collective-permute-done.5 = f32[128,1024]{1,0:T(8,128)S(1)} collective-permute-done((f32[128,1024]{1,0:T(8,128)S(1)}, f32[128,1024]{1,0:T(8,128)S(1)}, u32[]{:S(2)}, u32[]{:S(2)}) %collective-permute-start.5) | collective-permute-done | bytes 524320 | tf_op jit(solution)/shard_map/ppermute | solution.py:42
  34.2 2.9 %collective-permute-start.6 = (f32[1,128,1024]{2,1,0:T(8,128)S(1)}, f32[1,128,1024]{2,1,0:T(8,128)}, u32[]{:S(2)}, u32[]{:S(2)}) collective-permute-start(f32[1,128,1024]{2,1,0:T(8,128)S(1)} %bitcast.253), channel_id=1, source_target_pairs={{0,64},{1,65},{2,66},{3,67},{4,68},{5,69},{6,70},{7,71},{8,72},{9,... | collective-permute-start | bytes 1572872 | tf_op jit(solution)/shard_map/ppermute | solution.py:20
  39.0 2.3 %constant_dynamic-update-slice_fusion.4 = (f32[6,128,1024]{2,1,0:T(8,128)S(1)}, f32[1,128,1024]{2,1,0:T(8,128)S(1)}, f32[128,1024]{1,0:T(8,128)S(1)}, f32[128,1024]{1,0:T(8,128)S(1)}) fusion(f32[6,128,1024]{2,1,0:T(8,128)S(1)} %constant_dynamic-update-slice_fusion.5, f32[128,1024]{1,0:T(8,128)} %get-tuple-element.39, f32[128,1024]{1,0:T(8,128)} %copy-done.26, ...), kind=kLoop, calls=%fused_computation.133 | loop fusion | flops 786432 | bytes 5767168
  43.0 4.6 %collective-permute-start.8 = (f32[4,1,1024]{2,1,0:T(1,128)S(1)}, f32[4,1,1024]{2,1,0:T(1,128)S(1)}, u32[]{:S(2)}, u32[]{:S(2)}) collective-permute-start(f32[4,1,1024]{2,1,0:T(1,128)S(1)} %get-tuple-element.55), channel_id=1, source_target_pairs={{4,0},{8,4},{12,8},{16,12},{20,16},{24,20},{28,24},{32,28},{36,32}... | collective-permute-start | bytes 49160 | tf_op jit(solution)/shard_map/ppermute | solution.py:21
  47.6 1.9 collective-permute-start.9
  51.0 5.0 %collective-permute-start.11 = (f32[4,128,1]{2,1,0:T(8,128)S(1)}, f32[4,128,1]{2,1,0:T(8,128)S(1)}, u32[]{:S(2)}, u32[]{:S(2)}) collective-permute-start(f32[4,128,1]{2,1,0:T(8,128)S(1)} %get-tuple-element.53), channel_id=1, source_target_pairs={{0,1},{1,2},{2,3},{4,5},{5,6},{6,7},{8,9},{9,10},{10,11},{12,13},{... | collective-permute-start | bytes 6152 | tf_op jit(solution)/shard_map/ppermute | solution.py:20
  56.2 4.8 %collective-permute-done.10 = f32[4,128,1]{2,1,0:T(8,128)S(1)} collective-permute-done((f32[4,128,1]{2,1,0:T(8,128)S(1)}, f32[4,128,1]{2,1,0:T(8,128)S(1)}, u32[]{:S(2)}, u32[]{:S(2)}) %collective-permute-start.10) | collective-permute-done | bytes 2080 | tf_op jit(solution)/shard_map/ppermute | solution.py:21
  62.6 9.8 %multiply_reduce_fusion.2 = (f32[]{:T(128)}, f32[]{:T(128)}, f32[4,128,1024]{2,1,0:T(8,128)}) fusion(f32[1,128,1024]{2,1,0:T(8,128)S(1)} %bitcast.255, f32[1,128,1024]{2,1,0:T(8,128)S(1)} %bitcast.265, f32[1,128,1024]{2,1,0:T(8,128)S(1)} %bitcast.262, f32[1,128,1024]{2,1,0:T(8,128)S(1)} %get-tuple-element.33, f32[4,128,1024]{2,1,0:T(8,128)S(1)} %copy-done.8, ...), kind=kLoop, calls=%fused_computation.56 | loop fusion | flops 25690112 | bytes 25219080 | tf_op jit(solution)/shard_map/reduce_sum | solution.py:93
  75.9 2.4 %all-reduce.31 = (f32[2]{0:T(128)S(1)}, f32[2]{0:T(128)S(1)}) all-reduce(f32[2]{0:T(128)S(1)} %dynamic-update-slice, f32[2]{0:T(128)S(1)} %dynamic-update-slice.4), channel_id=1, replica_groups=mesh['layer'=2,'px_0'=4,'px_1'=4,'py'=4] {'layer'}, use_global_device_ids=true, to_apply=%add.8 | all-reduce | flops 4 | bytes 32
  82.9 8.6 %all-reduce.29 = (f32[4]{0:T(128)S(1)}, f32[4]{0:T(128)S(1)}) all-reduce(f32[4]{0:T(128)S(1)} %dynamic-update-slice.1, f32[4]{0:T(128)S(1)} %dynamic-update-slice.5), channel_id=1, replica_groups=mesh['layer'=2,'px_0'=4,'px_1'=4,'py'=4] {'px_0'}, use_global_device_ids=true, to_apply=%add.9 | all-reduce | flops 8 | bytes 64
  96.2 11.6 %all-reduce.27 = (f32[4]{0:T(128)S(1)}, f32[4]{0:T(128)S(1)}) all-reduce(f32[4]{0:T(128)S(1)} %dynamic-update-slice.2, f32[4]{0:T(128)S(1)} %dynamic-update-slice.6), channel_id=1, replica_groups=mesh['layer'=2,'px_0'=4,'px_1'=4,'py'=4] {'px_1'}, use_global_device_ids=true, to_apply=%add.10 | all-reduce | flops 8 | bytes 64
  111.7 12.3 %all-reduce.25 = (f32[4]{0:T(128)S(1)}, f32[4]{0:T(128)S(1)}) all-reduce(f32[4]{0:T(128)S(1)} %dynamic-update-slice.3, f32[4]{0:T(128)S(1)} %dynamic-update-slice.7), channel_id=1, replica_groups=mesh['layer'=2,'px_0'=4,'px_1'=4,'py'=4] {'py'}, use_global_device_ids=true, to_apply=%add.11 | all-reduce | flops 8 | bytes 64
  126.7 2.8 %multiply_subtract_fusion.1 = f32[4,128,1024]{2,1,0:T(8,128)S(1)} fusion(f32[4,128,1024]{2,1,0:T(8,128)} %param.6, f32[4,128,1024]{2,1,0:T(8,128)} %get-tuple-element.31, f32[]{:T(128)S(6)} %div.44), kind=kLoop, calls=%fused_computation.55 | loop fusion | flops 1048576 | bytes 6291460 | tf_op jit(solution)/shard_map/sub | solution.py:153
  135.5 2.5 %collective-permute-done.13 = f32[128,1024]{1,0:T(8,128)S(1)} collective-permute-done((f32[128,1024]{1,0:T(8,128)S(1)}, f32[128,1024]{1,0:T(8,128)S(1)}, u32[]{:S(2)}, u32[]{:S(2)}) %collective-permute-start.13) | collective-permute-done | bytes 524320 | tf_op jit(solution)/shard_map/ppermute | solution.py:42
  138.3 2.1 collective-permute-start.14
  144.1 2.6 %collective-permute-start.16 = (f32[4,1,1024]{2,1,0:T(1,128)S(1)}, f32[4,1,1024]{2,1,0:T(1,128)S(1)}, u32[]{:S(2)}, u32[]{:S(2)}) collective-permute-start(f32[4,1,1024]{2,1,0:T(1,128)S(1)} %get-tuple-element.51), channel_id=1, source_target_pairs={{4,0},{8,4},{12,8},{16,12},{20,16},{24,20},{28,24},{32,28},{36,32}... | collective-permute-start | bytes 49160 | tf_op jit(solution)/shard_map/ppermute | solution.py:21
  146.8 3.5 %collective-permute-start.17 = (f32[4,1,1024]{2,1,0:T(1,128)S(1)}, f32[4,1,1024]{2,1,0:T(1,128)S(1)}, u32[]{:S(2)}, u32[]{:S(2)}) collective-permute-start(f32[4,1,1024]{2,1,0:T(1,128)S(1)} %get-tuple-element.50), channel_id=1, source_target_pairs={{0,4},{4,8},{8,12},{12,16},{16,20},{20,24},{24,28},{28,32},{32,36}... | collective-permute-start | bytes 49160 | tf_op jit(solution)/shard_map/ppermute | solution.py:20
  151.8 4.6 %collective-permute-start.19 = (f32[4,128,1]{2,1,0:T(8,128)S(1)}, f32[4,128,1]{2,1,0:T(8,128)S(1)}, u32[]{:S(2)}, u32[]{:S(2)}) collective-permute-start(f32[4,128,1]{2,1,0:T(8,128)S(1)} %get-tuple-element.49), channel_id=1, source_target_pairs={{0,1},{1,2},{2,3},{4,5},{5,6},{6,7},{8,9},{9,10},{10,11},{12,13},{... | collective-permute-start | bytes 6152 | tf_op jit(solution)/shard_map/ppermute | solution.py:20
  156.5 4.7 %collective-permute-done.18 = f32[4,128,1]{2,1,0:T(8,128)S(1)} collective-permute-done((f32[4,128,1]{2,1,0:T(8,128)S(1)}, f32[4,128,1]{2,1,0:T(8,128)S(1)}, u32[]{:S(2)}, u32[]{:S(2)}) %collective-permute-start.18) | collective-permute-done | bytes 2080 | tf_op jit(solution)/shard_map/ppermute | solution.py:21
  162.4 8.5 %multiply_reduce_fusion = (f32[]{:T(128)}, f32[]{:T(128)}, f32[4,128,1024]{2,1,0:T(8,128)}) fusion(f32[1,128,1024]{2,1,0:T(8,128)S(1)} %bitcast.259, f32[1,128,1024]{2,1,0:T(8,128)S(1)} %bitcast.271, f32[1,128,1024]{2,1,0:T(8,128)S(1)} %bitcast.268, f32[1,128,1024]{2,1,0:T(8,128)S(1)} %get-tuple-element.24, f32[4,128,1024]{2,1,0:T(8,128)S(1)} %multiply_subtract_fusion.1, ...), kind=kLoop, calls=%fused_computation.53 | loop fusion | flops 25690112 | bytes 25219080 | tf_op jit(solution)/shard_map/reduce_sum | solution.py:93
  173.8 2.4 %all-reduce.30 = (f32[2]{0:T(128)S(1)}, f32[2]{0:T(128)S(1)}) all-reduce(f32[2]{0:T(128)S(1)} %dynamic-update-slice.8, f32[2]{0:T(128)S(1)} %dynamic-update-slice.12), channel_id=1, replica_groups=mesh['layer'=2,'px_0'=4,'px_1'=4,'py'=4] {'layer'}, use_global_device_ids=true, to_apply=%add.16 | all-reduce | flops 4 | bytes 32
  180.3 8.8 %all-reduce.28 = (f32[4]{0:T(128)S(1)}, f32[4]{0:T(128)S(1)}) all-reduce(f32[4]{0:T(128)S(1)} %dynamic-update-slice.9, f32[4]{0:T(128)S(1)} %dynamic-update-slice.13), channel_id=1, replica_groups=mesh['layer'=2,'px_0'=4,'px_1'=4,'py'=4] {'px_0'}, use_global_device_ids=true, to_apply=%add.17 | all-reduce | flops 8 | bytes 64
  193.3 9.7 %all-reduce.26 = (f32[4]{0:T(128)S(1)}, f32[4]{0:T(128)S(1)}) all-reduce(f32[4]{0:T(128)S(1)} %dynamic-update-slice.10, f32[4]{0:T(128)S(1)} %dynamic-update-slice.14), channel_id=1, replica_groups=mesh['layer'=2,'px_0'=4,'px_1'=4,'py'=4] {'px_1'}, use_global_device_ids=true, to_apply=%add.18 | all-reduce | flops 8 | bytes 64
  207.1 10.2 %all-reduce.24 = (f32[4]{0:T(128)S(1)}, f32[4]{0:T(128)S(1)}) all-reduce(f32[4]{0:T(128)S(1)} %dynamic-update-slice.11, f32[4]{0:T(128)S(1)} %dynamic-update-slice.15), channel_id=1, replica_groups=mesh['layer'=2,'px_0'=4,'px_1'=4,'py'=4] {'py'}, use_global_device_ids=true, to_apply=%add.19 | all-reduce | flops 8 | bytes 64
  223.0 6.0 %multiply_subtract_fusion = (f32[4,128,1024]{2,1,0:T(8,128)}, f32[4,128,1024]{2,1,0:T(8,128)}) fusion(f32[4,128,1024]{2,1,0:T(8,128)} %copy-done.6, f32[4,128,1024]{2,1,0:T(8,128)} %get-tuple-element.22, f32[4,128,1024]{2,1,0:T(8,128)} %get-tuple-element.31, f32[]{:T(128)S(6)} %div.45, f32[]{:T(128)S(6)} %div.47, f32[1,128,1024]{2,1,0:T(8,128)} %bitcast.260, ...), kind=kLoop, calls=%fused_computation.51 | loop fusion | flops 7864320 | bytes 14680076 | tf_op jit(solution)/shard_map/sub | solution.py:153
  (190 shorter events, 63.2 us)
Async XLA Ops:
  3.8 14.2 %collective-permute-start = (f32[1,128,1024]{2,1,0:T(8,128)S(1)}, f32[1,128,1024]{2,1,0:T(8,128)S(1)}, u32[]{:S(2)}, u32[]{:S(2)}) collective-permute-start(f32[1,128,1024]{2,1,0:T(8,128)S(1)} %slice.202), channel_id=1, source_target_pairs={{0,64},{1,65},{2,66},{3,67},{4,68},{5,69},{6,70},{7,71},{8,72},{9,... | collective-permute-start | bytes 1572872 | tf_op jit(solution)/shard_map/ppermute | solution.py:42
  5.8 12.3 %collective-permute-start.1 = (f32[4,1,1024]{2,1,0:T(1,128)S(1)}, f32[4,1,1024]{2,1,0:T(1,128)S(1)}, u32[]{:S(2)}, u32[]{:S(2)}) collective-permute-start(f32[4,1,1024]{2,1,0:T(1,128)S(1)} %slice.173), channel_id=1, source_target_pairs={{0,4},{4,8},{8,12},{12,16},{16,20},{20,24},{24,28},{28,32},{32,36}... | collective-permute-start | bytes 49160 | tf_op jit(solution)/shard_map/ppermute | solution.py:42
  9.7 8.3 %collective-permute-start.2 = (f32[4,128,1]{2,1,0:T(8,128)S(1)}, f32[4,128,1]{2,1,0:T(8,128)S(1)}, u32[]{:S(2)}, u32[]{:S(2)}) collective-permute-start(f32[4,128,1]{2,1,0:T(8,128)S(1)} %slice.175), channel_id=1, source_target_pairs={{0,1},{1,2},{2,3},{4,5},{5,6},{6,7},{8,9},{9,10},{10,11},{12,13},{... | collective-permute-start | bytes 6152 | tf_op jit(solution)/shard_map/ppermute | solution.py:42
  20.3 2.9 %collective-permute-start.3 = (f32[128,1024]{1,0:T(8,128)S(1)}, f32[128,1024]{1,0:T(8,128)S(1)}, u32[]{:S(2)}, u32[]{:S(2)}) collective-permute-start(f32[128,1024]{1,0:T(8,128)S(1)} %fusion.30), channel_id=1, source_target_pairs={{0,64},{1,65},{2,66},{3,67},{4,68},{5,69},{6,70},{7,71},{8,72},{9,... | collective-permute-start | bytes 1572872 | tf_op jit(solution)/shard_map/ppermute | solution.py:42
  24.1 3.8 %collective-permute-start.4 = (f32[128,1024]{1,0:T(8,128)S(1)}, f32[128,1024]{1,0:T(8,128)S(1)}, u32[]{:S(2)}, u32[]{:S(2)}) collective-permute-start(f32[128,1024]{1,0:T(8,128)S(1)} %get-tuple-element.40), channel_id=1, source_target_pairs={{0,64},{1,65},{2,66},{3,67},{4,68},{5,69},{6,70},{7,71},{8,72},{9,... | collective-permute-start | bytes 1572872 | tf_op jit(solution)/shard_map/ppermute | solution.py:42
  29.9 3.9 %collective-permute-start.5 = (f32[128,1024]{1,0:T(8,128)S(1)}, f32[128,1024]{1,0:T(8,128)S(1)}, u32[]{:S(2)}, u32[]{:S(2)}) collective-permute-start(f32[128,1024]{1,0:T(8,128)S(1)} %get-tuple-element.36), channel_id=1, source_target_pairs={{64,0},{65,1},{66,2},{67,3},{68,4},{69,5},{70,6},{71,7},{72,8},{73... | collective-permute-start | bytes 1572872 | tf_op jit(solution)/shard_map/ppermute | solution.py:42
  34.2 3.7 %collective-permute-start.6 = (f32[1,128,1024]{2,1,0:T(8,128)S(1)}, f32[1,128,1024]{2,1,0:T(8,128)}, u32[]{:S(2)}, u32[]{:S(2)}) collective-permute-start(f32[1,128,1024]{2,1,0:T(8,128)S(1)} %bitcast.253), channel_id=1, source_target_pairs={{0,64},{1,65},{2,66},{3,67},{4,68},{5,69},{6,70},{7,71},{8,72},{9,... | collective-permute-start | bytes 1572872 | tf_op jit(solution)/shard_map/ppermute | solution.py:20
  39.0 23.6 %copy-start.13 = (f32[4,128,1024]{2,1,0:T(8,128)S(1)}, f32[4,128,1024]{2,1,0:T(8,128)}, u32[]{:S(2)}) copy-start(f32[4,128,1024]{2,1,0:T(8,128)} %param.11) | copy-start | bytes 6291460
  41.3 21.3 %copy-start.18 = (f32[128,1024]{1,0:T(8,128)}, f32[128,1024]{1,0:T(8,128)S(1)}, u32[]{:S(2)}) copy-start(f32[128,1024]{1,0:T(8,128)S(1)} %get-tuple-element.34) | copy-start | bytes 1572868
  41.4 21.2 %copy-start.19 = (f32[128,1024]{1,0:T(8,128)}, f32[128,1024]{1,0:T(8,128)S(1)}, u32[]{:S(2)}) copy-start(f32[128,1024]{1,0:T(8,128)S(1)} %get-tuple-element.35) | copy-start | bytes 1572868
  41.4 21.2 %copy-start.28 = (f32[1,128,1024]{2,1,0:T(8,128)}, f32[1,128,1024]{2,1,0:T(8,128)S(1)}, u32[]{:S(2)}) copy-start(f32[1,128,1024]{2,1,0:T(8,128)S(1)} %get-tuple-element.33) | copy-start | bytes 1572868
  41.4 14.7 %collective-permute-start.7 = (f32[1,128,1024]{2,1,0:T(8,128)S(1)}, f32[1,128,1024]{2,1,0:T(8,128)S(1)}, u32[]{:S(2)}, u32[]{:S(2)}) collective-permute-start(f32[1,128,1024]{2,1,0:T(8,128)S(1)} %get-tuple-element.33), channel_id=1, source_target_pairs={{64,0},{65,1},{66,2},{67,3},{68,4},{69,5},{70,6},{71,7},{72,8},{73... | collective-permute-start | bytes 1572872 | tf_op jit(solution)/shard_map/ppermute | solution.py:21
  42.7 19.9 %copy-start.10 = (f32[3,128,1024]{2,1,0:T(8,128)S(1)}, f32[3,128,1024]{2,1,0:T(8,128)}, u32[]{:S(2)}) copy-start(f32[3,128,1024]{2,1,0:T(8,128)} %copy-done.9) | copy-start | bytes 4718596
  43.0 13.0 %collective-permute-start.8 = (f32[4,1,1024]{2,1,0:T(1,128)S(1)}, f32[4,1,1024]{2,1,0:T(1,128)S(1)}, u32[]{:S(2)}, u32[]{:S(2)}) collective-permute-start(f32[4,1,1024]{2,1,0:T(1,128)S(1)} %get-tuple-element.55), channel_id=1, source_target_pairs={{4,0},{8,4},{12,8},{16,12},{20,16},{24,20},{28,24},{32,28},{36,32}... | collective-permute-start | bytes 49160 | tf_op jit(solution)/shard_map/ppermute | solution.py:21
  47.6 8.5 %collective-permute-start.9 = (f32[4,1,1024]{2,1,0:T(1,128)S(1)}, f32[4,1,1024]{2,1,0:T(1,128)S(1)}, u32[]{:S(2)}, u32[]{:S(2)}) collective-permute-start(f32[4,1,1024]{2,1,0:T(1,128)S(1)} %get-tuple-element.54), channel_id=1, source_target_pairs={{0,4},{4,8},{8,12},{12,16},{16,20},{20,24},{24,28},{28,32},{32,36}... | collective-permute-start | bytes 49160 | tf_op jit(solution)/shard_map/ppermute | solution.py:20
  49.7 11.4 %collective-permute-start.10 = (f32[4,128,1]{2,1,0:T(8,128)S(1)}, f32[4,128,1]{2,1,0:T(8,128)S(1)}, u32[]{:S(2)}, u32[]{:S(2)}) collective-permute-start(f32[4,128,1]{2,1,0:T(8,128)S(1)} %get-tuple-element.52), channel_id=1, source_target_pairs={{1,0},{2,1},{3,2},{5,4},{6,5},{7,6},{9,8},{10,9},{11,10},{13,12},{... | collective-permute-start | bytes 6152 | tf_op jit(solution)/shard_map/ppermute | solution.py:21
  51.0 11.6 %collective-permute-start.11 = (f32[4,128,1]{2,1,0:T(8,128)S(1)}, f32[4,128,1]{2,1,0:T(8,128)S(1)}, u32[]{:S(2)}, u32[]{:S(2)}) collective-permute-start(f32[4,128,1]{2,1,0:T(8,128)S(1)} %get-tuple-element.53), channel_id=1, source_target_pairs={{0,1},{1,2},{2,3},{4,5},{5,6},{6,7},{8,9},{9,10},{10,11},{12,13},{... | collective-permute-start | bytes 6152 | tf_op jit(solution)/shard_map/ppermute | solution.py:20
  56.2 26.1 %copy-start.38 = (u32[128]{0:T(128)S(1)}, u32[128]{0:T(128)}, u32[]{:S(2)}) copy-start(u32[128]{0:T(128)} %constant.45) | copy-start | bytes 1540
  56.2 39.4 %copy-start.37 = (u32[128]{0:T(128)S(1)}, u32[128]{0:T(128)}, u32[]{:S(2)}) copy-start(u32[128]{0:T(128)} %constant.50) | copy-start | bytes 1540
  129.5 32.8 %copy-start.6 = (f32[4,128,1024]{2,1,0:T(8,128)}, f32[4,128,1024]{2,1,0:T(8,128)S(1)}, u32[]{:S(2)}) copy-start(f32[4,128,1024]{2,1,0:T(8,128)S(1)} %multiply_subtract_fusion.1) | copy-start | bytes 6291460
  130.3 2.9 %collective-permute-start.12 = (f32[128,1024]{1,0:T(8,128)S(1)}, f32[128,1024]{1,0:T(8,128)S(1)}, u32[]{:S(2)}, u32[]{:S(2)}) collective-permute-start(f32[128,1024]{1,0:T(8,128)S(1)} %add_multiply_fusion.3), channel_id=1, source_target_pairs={{0,64},{1,65},{2,66},{3,67},{4,68},{5,69},{6,70},{7,71},{8,72},{9,... | collective-permute-start | bytes 1572872 | tf_op jit(solution)/shard_map/ppermute | solution.py:42
  134.2 3.8 %collective-permute-start.13 = (f32[128,1024]{1,0:T(8,128)S(1)}, f32[128,1024]{1,0:T(8,128)S(1)}, u32[]{:S(2)}, u32[]{:S(2)}) collective-permute-start(f32[128,1024]{1,0:T(8,128)S(1)} %get-tuple-element.27), channel_id=1, source_target_pairs={{64,0},{65,1},{66,2},{67,3},{68,4},{69,5},{70,6},{71,7},{72,8},{73... | collective-permute-start | bytes 1572872 | tf_op jit(solution)/shard_map/ppermute | solution.py:42
  138.3 24.0 %copy-start.15 = (f32[128,1024]{1,0:T(8,128)}, f32[128,1024]{1,0:T(8,128)S(1)}, u32[]{:S(2)}) copy-start(f32[128,1024]{1,0:T(8,128)S(1)} %multiply_add_fusion.3) | copy-start | bytes 1572868
  138.3 3.6 %collective-permute-start.14 = (f32[1,128,1024]{2,1,0:T(8,128)S(1)}, f32[1,128,1024]{2,1,0:T(8,128)S(1)}, u32[]{:S(2)}, u32[]{:S(2)}) collective-permute-start(f32[1,128,1024]{2,1,0:T(8,128)S(1)} %bitcast.257), channel_id=1, source_target_pairs={{0,64},{1,65},{2,66},{3,67},{4,68},{5,69},{6,70},{7,71},{8,72},{9,... | collective-permute-start | bytes 1572872 | tf_op jit(solution)/shard_map/ppermute | solution.py:20
  142.5 19.9 %copy-start.20 = (f32[128,1024]{1,0:T(8,128)}, f32[128,1024]{1,0:T(8,128)S(1)}, u32[]{:S(2)}) copy-start(f32[128,1024]{1,0:T(8,128)S(1)} %get-tuple-element.25) | copy-start | bytes 1572868
  142.5 19.9 %copy-start.21 = (f32[128,1024]{1,0:T(8,128)}, f32[128,1024]{1,0:T(8,128)S(1)}, u32[]{:S(2)}) copy-start(f32[128,1024]{1,0:T(8,128)S(1)} %get-tuple-element.26) | copy-start | bytes 1572868
  142.5 19.9 %copy-start.29 = (f32[1,128,1024]{2,1,0:T(8,128)}, f32[1,128,1024]{2,1,0:T(8,128)S(1)}, u32[]{:S(2)}) copy-start(f32[1,128,1024]{2,1,0:T(8,128)S(1)} %get-tuple-element.24) | copy-start | bytes 1572868
  142.5 13.9 %collective-permute-start.15 = (f32[1,128,1024]{2,1,0:T(8,128)S(1)}, f32[1,128,1024]{2,1,0:T(8,128)S(1)}, u32[]{:S(2)}, u32[]{:S(2)}) collective-permute-start(f32[1,128,1024]{2,1,0:T(8,128)S(1)} %get-tuple-element.24), channel_id=1, source_target_pairs={{64,0},{65,1},{66,2},{67,3},{68,4},{69,5},{70,6},{71,7},{72,8},{73... | collective-permute-start | bytes 1572872 | tf_op jit(solution)/shard_map/ppermute | solution.py:21
  144.1 12.2 %collective-permute-start.16 = (f32[4,1,1024]{2,1,0:T(1,128)S(1)}, f32[4,1,1024]{2,1,0:T(1,128)S(1)}, u32[]{:S(2)}, u32[]{:S(2)}) collective-permute-start(f32[4,1,1024]{2,1,0:T(1,128)S(1)} %get-tuple-element.51), channel_id=1, source_target_pairs={{4,0},{8,4},{12,8},{16,12},{20,16},{24,20},{28,24},{32,28},{36,32}... | collective-permute-start | bytes 49160 | tf_op jit(solution)/shard_map/ppermute | solution.py:21
  146.8 9.6 %collective-permute-start.17 = (f32[4,1,1024]{2,1,0:T(1,128)S(1)}, f32[4,1,1024]{2,1,0:T(1,128)S(1)}, u32[]{:S(2)}, u32[]{:S(2)}) collective-permute-start(f32[4,1,1024]{2,1,0:T(1,128)S(1)} %get-tuple-element.50), channel_id=1, source_target_pairs={{0,4},{4,8},{8,12},{12,16},{16,20},{20,24},{24,28},{28,32},{32,36}... | collective-permute-start | bytes 49160 | tf_op jit(solution)/shard_map/ppermute | solution.py:20
  150.5 10.7 %collective-permute-start.18 = (f32[4,128,1]{2,1,0:T(8,128)S(1)}, f32[4,128,1]{2,1,0:T(8,128)S(1)}, u32[]{:S(2)}, u32[]{:S(2)}) collective-permute-start(f32[4,128,1]{2,1,0:T(8,128)S(1)} %get-tuple-element.48), channel_id=1, source_target_pairs={{1,0},{2,1},{3,2},{5,4},{6,5},{7,6},{9,8},{10,9},{11,10},{13,12},{... | collective-permute-start | bytes 6152 | tf_op jit(solution)/shard_map/ppermute | solution.py:21
  151.8 10.6 %collective-permute-start.19 = (f32[4,128,1]{2,1,0:T(8,128)S(1)}, f32[4,128,1]{2,1,0:T(8,128)S(1)}, u32[]{:S(2)}, u32[]{:S(2)}) collective-permute-start(f32[4,128,1]{2,1,0:T(8,128)S(1)} %get-tuple-element.49), channel_id=1, source_target_pairs={{0,1},{1,2},{2,3},{4,5},{5,6},{6,7},{8,9},{9,10},{10,11},{12,13},{... | collective-permute-start | bytes 6152 | tf_op jit(solution)/shard_map/ppermute | solution.py:20
  (29 other events, 269.0 us)
